TPU v7x, 1024 devices: a whole 8x8x8 slice. The times are simulated.
1024 devices in a mesh: dp: 16 (over x, core), expert: 64 (over z, y).
Axes of the slice: x: 8, y: 8, z: 8, core: 2. Of those that a mesh axis runs over, the one named last changes fastest.
Arguments:
- tokens: bfloat16 [16384, 2048], P(('dp', 'expert')), may hold values from -24 to 24
- out_grad: bfloat16 [16384, 2048], P(('dp', 'expert')), may hold values from -24 to 24
- expert_ids: int32 [16384, 8], P(('dp', 'expert')), may hold values from 0 to 63, all different within a row; in each aligned block of 16 rows (0 to 15, 16 to 31, ...) at most 4 rows name the same one
- probs: bfloat16 [16384, 8], P(('dp', 'expert')), may hold values from 0.049804688 to 0.5
- w_gate: bfloat16 [64, 2048, 384], P('expert'), may hold values from -0.125 to 0.125
- w_up: bfloat16 [64, 2048, 384], P('expert'), may hold values from -0.125 to 0.125
- w_down: bfloat16 [64, 2048, 384], P('expert'), may hold values from -0.3125 to 0.3125
Outputs:
- token_grad: bfloat16 [16384, 2048], P(('dp', 'expert'))
- prob_grad: bfloat16 [16384, 8], P(('dp', 'expert'))
- gate_grad: float32 [64, 2048, 384], P('expert', 'dp')
- up_grad: float32 [64, 2048, 384], P('expert', 'dp')
- down_grad: float32 [64, 2048, 384], P('expert', 'dp')
Inputs may be any that keep to these rules, and one draw needn't show every extreme that they name: `expert_ids`: each row names 8 different experts. Within each aligned block of 16 rows (the rows of one device) no expert is named by more than 4 rows, and that bound is reached in some blocks.
All inputs are finite; a program needn't handle non-finite values.
Results may differ from a plain program's by a relative error of at most 0.017.
Values may be sent and summed in bfloat16 or wider, within the bound.
A program may use at most 64 MiB of HBM per device.

v0:
```python
import math

import jax
import jax.numpy as jnp
from jax import lax
from jax.sharding import PartitionSpec as P


def side_by_side(arrays, axis, split_dim, concat_dim, along):
    widths = [math.prod(a.shape[along:]) for a in arrays]
    both = jnp.concatenate(
        [a.reshape(*a.shape[:along], w) for a, w in zip(arrays, widths)], axis=along
    )
    whole = lax.all_to_all(both, axis, split_axis=split_dim, concat_axis=concat_dim, tiled=True)
    pieces = jnp.split(whole, [sum(widths[:k]) for k in range(1, len(widths))], axis=along)
    return tuple(
        (b.reshape(*whole.shape[:along], *a.shape[along:]) for a, b in zip(arrays, pieces))
    )


def body(tokens, out_grad, expert_ids, probs, w_gate, w_up, w_down):
    tok_rows, width = tokens.shape
    top = expert_ids.shape[1]
    local = w_gate.shape[0]
    hidden_units = w_gate.shape[2]
    ranks = lax.axis_size("expert")
    experts = local * ranks
    slots = 2 * tok_rows * top // experts
    flat = expert_ids.reshape(-1)
    onehot = (flat[:, None] == jnp.arange(experts, dtype=jnp.int32)[None, :]).astype(jnp.int32)
    before = jnp.cumsum(onehot, axis=0) - onehot
    place = jnp.sum(before * onehot, axis=1)
    target = flat * slots + place
    select = jnp.arange(experts * slots, dtype=jnp.int32)[:, None] == target[None, :]
    by_token = jnp.any(select.reshape(experts * slots, tok_rows, top), axis=2).astype(jnp.bfloat16)
    sent_x = jnp.dot(by_token, tokens, preferred_element_type=jnp.float32).astype(jnp.bfloat16)
    sent_dy = jnp.dot(by_token, out_grad, preferred_element_type=jnp.float32).astype(jnp.bfloat16)
    sent_p = jnp.sum(
        jnp.where(select, probs.reshape(-1)[None, :].astype(jnp.float32), 0.0), axis=1
    ).astype(jnp.bfloat16)
    sent_x = sent_x.reshape(ranks, local, slots, width)
    sent_dy = sent_dy.reshape(ranks, local, slots, width)
    sent_p = sent_p.reshape(ranks, local, slots)
    expert_rows_x = lax.all_to_all(sent_x, "expert", split_axis=0, concat_axis=0, tiled=True)
    rows_dy = lax.all_to_all(sent_dy, "expert", split_axis=0, concat_axis=0, tiled=True)
    rows_p = lax.all_to_all(sent_p, "expert", split_axis=0, concat_axis=0, tiled=True)
    gate_pre = jnp.einsum(
        "sjcd,jdf->sjcf", expert_rows_x, w_gate, preferred_element_type=jnp.float32
    )
    up_pre = jnp.einsum("sjcd,jdf->sjcf", expert_rows_x, w_up, preferred_element_type=jnp.float32)
    sigma = jax.nn.sigmoid(gate_pre)
    silu = gate_pre * sigma
    expert_act = (silu * up_pre).astype(jnp.bfloat16)
    expert_scaled = (rows_p.astype(jnp.float32)[..., None] * rows_dy.astype(jnp.float32)).astype(
        jnp.bfloat16
    )
    expert_out = jnp.einsum(
        "sjcf,jdf->sjcd", expert_act, w_down, preferred_element_type=jnp.float32
    )
    prob_back = jnp.sum(rows_dy.astype(jnp.float32) * expert_out, axis=3).astype(jnp.bfloat16)
    act_grad = jnp.einsum(
        "sjcd,jdf->sjcf", expert_scaled, w_down, preferred_element_type=jnp.float32
    )
    expert_gate_back = (act_grad * up_pre * sigma * (1.0 + gate_pre * (1.0 - sigma))).astype(
        jnp.bfloat16
    )
    expert_up_back = (act_grad * silu).astype(jnp.bfloat16)
    contrib = (
        jnp.einsum("sjcf,jdf->sjcd", expert_gate_back, w_gate, preferred_element_type=jnp.float32)
        + jnp.einsum("sjcf,jdf->sjcd", expert_up_back, w_up, preferred_element_type=jnp.float32)
    ).astype(jnp.bfloat16)
    contrib, prob_back, rows_x, scaled, act, gate_back, up_back = (
        contrib,
        prob_back,
        expert_rows_x,
        expert_scaled,
        expert_act,
        expert_gate_back,
        expert_up_back,
    )
    back_rows, back_prob = side_by_side((contrib, prob_back), "expert", 0, 0, 3)
    back_rows = back_rows.reshape(experts * slots, width)
    back_prob = back_prob.reshape(experts * slots)
    token_grad = jnp.einsum(
        "et,ed->td", by_token, back_rows, preferred_element_type=jnp.float32
    ).astype(jnp.bfloat16)
    prob_grad = jnp.sum(jnp.where(select, back_prob[:, None].astype(jnp.float32), 0.0), axis=0)
    prob_grad = prob_grad.reshape(tok_rows, top).astype(jnp.bfloat16)
    groups = lax.axis_size("dp")
    share = width // groups
    part_gate = jnp.einsum("sjcd,sjcf->djf", rows_x, gate_back, preferred_element_type=jnp.float32)
    part_up = jnp.einsum("sjcd,sjcf->djf", rows_x, up_back, preferred_element_type=jnp.float32)
    part_down = jnp.einsum("sjcd,sjcf->djf", scaled, act, preferred_element_type=jnp.float32)
    summed = lax.psum_scatter(
        jnp.stack((part_gate, part_up, part_down), axis=1)
        .reshape(share * lax.axis_size("dp"), 3 * local * hidden_units)
        .astype(jnp.bfloat16),
        "dp",
        scatter_dimension=0,
        tiled=True,
    ).astype(jnp.float32)
    summed = jnp.transpose(summed.reshape(share, 3, local, hidden_units), (1, 2, 0, 3))
    gate_grad, up_grad, down_grad = (summed[0], summed[1], summed[2])
    return (token_grad, prob_grad, gate_grad, up_grad, down_grad)


def solution(mesh):
    placed = (
        P(("dp", "expert"), None),
        P(("dp", "expert"), None),
        P(("dp", "expert"), None),
        P(("dp", "expert"), None),
        P("expert", None, None),
        P("expert", None, None),
        P("expert", None, None),
    )
    return jax.shard_map(
        body,
        mesh=mesh,
        in_specs=placed,
        out_specs=(
            P(("dp", "expert"), None),
            P(("dp", "expert"), None),
            P("expert", "dp", None),
            P("expert", "dp", None),
            P("expert", "dp", None),
        ),
        check_vma=False,
    )
```

profile of v0, /device:TPU:1, one launch (start us, length us, event | category | flops | bytes accessed | tf_op | source)
XLA Modules:
  0.0 210.3 jit_solution(3588073758382980653)
XLA Ops:
  7.2 0.9 copy.46
  8.1 0.1 eq.36
  8.1 0.1 fusion.46
  8.2 0.2 reduce_window_sum.11
  8.4 0.2 select_reduce_fusion.2
  8.6 0.8 copy.48
  9.5 0.1 select_reduce_fusion.1
  9.6 0.7 convert_element_type.129
  10.3 23.9 %all-to-all-start = ((bf16[64,1,4]{2,1,0:T(2,128)(2,1)}), bf16[64,1,4]{2,1,0:T(2,128)(2,1)S(1)}, u32[]{:S(2)}, u32[]{:S(2)}) async-start(bf16[64,1,4]{2,1,0:T(2,128)(2,1)} %convert_element_type.129), calls=%async_computation | async-start | bytes 65536 | tf_op jit(solution)/shard_map/all_to_all | solution.py:46
  34.4 0.1 fusion.45
  34.5 1.3 convolution_convert_fusion
  35.8 1.2 reshape.145
  37.0 8.0 %all-to-all-done = bf16[64,1,4]{2,1,0:T(2,128)(2,1)S(1)} async-done(((bf16[64,1,4]{2,1,0:T(2,128)(2,1)}), bf16[64,1,4]{2,1,0:T(2,128)(2,1)S(1)}, u32[]{:S(2)}, u32[]{:S(2)}) %all-to-all-start) | async-done | bytes 544 | tf_op jit(solution)/shard_map/all_to_all | solution.py:46
  45.1 5.5 %all-to-all-start.2 = ((bf16[64,1,4,2048]{3,2,1,0:T(4,128)(2,1)}), bf16[64,1,4,2048]{3,2,1,0:T(4,128)(2,1)}, u32[]{:S(2)}, u32[]{:S(2)}) async-start(bf16[64,1,4,2048]{3,2,1,0:T(4,128)(2,1)} %bitcast.8), calls=%async_computation.2 | async-start | bytes 2097152 | tf_op jit(solution)/shard_map/all_to_all | solution.py:44
  50.6 0.5 convolution_convert_fusion.1
  51.1 1.2 reshape.142
  52.3 24.0 %all-to-all-done.2 = bf16[64,1,4,2048]{3,2,1,0:T(4,128)(2,1)} async-done(((bf16[64,1,4,2048]{3,2,1,0:T(4,128)(2,1)}), bf16[64,1,4,2048]{3,2,1,0:T(4,128)(2,1)}, u32[]{:S(2)}, u32[]{:S(2)}) %all-to-all-start.2) | async-done | bytes 1048608 | tf_op jit(solution)/shard_map/all_to_all | solution.py:44
  76.3 8.9 %all-to-all-start.1 = ((bf16[64,1,4,2048]{3,2,1,0:T(4,128)(2,1)}), bf16[64,1,4,2048]{3,2,1,0:T(4,128)(2,1)}, u32[]{:S(2)}, u32[]{:S(2)}) async-start(bf16[64,1,4,2048]{3,2,1,0:T(4,128)(2,1)} %bitcast.1), calls=%async_computation.1 | async-start | bytes 2097152 | tf_op jit(solution)/shard_map/all_to_all | solution.py:45
  85.2 0.2 reduce-scatter.4.cloned.1.call-start
  85.6 3.1 %fusion.26 = f32[64,1,4,384]{3,0,2,1:T(8,128)} fusion(bf16[1,2048,384]{2,1,0:T(8,128)(2,1)S(1)} %copy-done, bf16[64,1,4,2048]{3,2,1,0:T(4,128)(2,1)} %all-to-all-done.2), kind=kOutput, calls=%fused_computation.30 | convolution fusion | flops 402653184 | bytes 3014656 | tf_op jit(solution)/shard_map/sjcd,jdf->sjcf/dot_general | solution.py:47
  88.6 2.9 %fusion.23 = f32[64,1,4,384]{3,0,2,1:T(8,128)} fusion(bf16[1,2048,384]{2,1,0:T(8,128)(2,1)S(1)} %copy-done.1, bf16[64,1,4,2048]{3,2,1,0:T(4,128)(2,1)} %all-to-all-done.2), kind=kOutput, calls=%fused_computation.29 | convolution fusion | flops 402653184 | bytes 3014656 | tf_op jit(solution)/shard_map/sjcd,jdf->sjcf/dot_general | solution.py:50
  91.6 19.2 %all-to-all-done.1 = bf16[64,1,4,2048]{3,2,1,0:T(4,128)(2,1)} async-done(((bf16[64,1,4,2048]{3,2,1,0:T(4,128)(2,1)}), bf16[64,1,4,2048]{3,2,1,0:T(4,128)(2,1)}, u32[]{:S(2)}, u32[]{:S(2)}) %all-to-all-start.1) | async-done | bytes 1048608 | tf_op jit(solution)/shard_map/all_to_all | solution.py:45
  110.8 3.1 %fusion.41 = (bf16[64,4,384]{2,0,1:T(8,128)(2,1)S(1)}, bf16[64,1,4,384]{3,0,2,1:T(8,128)(2,1)S(1)}, bf16[64,4,384]{2,0,1:T(8,128)(2,1)S(1)}) fusion(f32[64,1,4,384]{3,0,2,1:T(8,128)} %fusion.26, f32[64,1,4,384]{3,0,2,1:T(8,128)} %fusion.23, bf16[1,2048,384]{2,1,0:T(8,128)(2,1)} %param.13, f32[64,4]{0,1:T(4,128)S(1)} %copy.50, ...), kind=kOutput, calls=%fused_computation.47 | convolution fusion | flops 405700608 | bytes 3998720 | tf_op jit(solution)/shard_map/sjcd,jdf->sjcf/dot_general | solution.py:61
  113.9 2.9 %fusion.3 = bf16[2048,1,1,384]{0,3,2,1:T(8,128)(2,1)S(1)} fusion(bf16[64,4,384]{2,0,1:T(8,128)(2,1)S(1)} %get-tuple-element.27, f32[64,4]{0,1:T(4,128)S(1)} %copy.50, bf16[64,1,4,2048]{3,2,1,0:T(4,128)(2,1)} %all-to-all-done.1), kind=kOutput, calls=%fused_computation.10 | convolution fusion | flops 405012480 | bytes 2819072 | tf_op jit(solution)/shard_map/sjcd,sjcf->djf/dot_general | solution.py:93
  116.8 2.7 %fusion.2 = bf16[2048,1,1,384]{0,3,2,1:T(8,128)(2,1)S(1)} fusion(bf16[64,4,384]{2,0,1:T(8,128)(2,1)S(1)} %get-tuple-element.25, bf16[64,1,4,2048]{3,2,1,0:T(4,128)(2,1)} %all-to-all-done.2), kind=kOutput, calls=%fused_computation.9 | convolution fusion | flops 403439616 | bytes 2818048 | tf_op jit(solution)/shard_map/sjcd,sjcf->djf/dot_general | solution.py:92
  119.5 2.7 %fusion.1 = bf16[2048,1,1,384]{0,3,2,1:T(8,128)(2,1)S(1)} fusion(bf16[64,1,4,2048]{3,2,1,0:T(4,128)(2,1)} %all-to-all-done.2, bf16[64,1,4,384]{3,0,2,1:T(8,128)(2,1)S(1)} %get-tuple-element.26), kind=kOutput, calls=%fused_computation.8 | convolution fusion | flops 403439616 | bytes 2818048 | tf_op jit(solution)/shard_map/sjcd,sjcf->djf/dot_general | solution.py:91
  122.3 2.4 %pad_maximum_fusion = bf16[2048,3,1,384]{0,3,2,1:T(8,128)(2,1)} fusion(bf16[2048,1,1,384]{0,3,2,1:T(8,128)(2,1)S(1)} %fusion.3, bf16[2048,1,1,384]{0,3,2,1:T(8,128)(2,1)S(1)} %fusion.2, bf16[2048,1,1,384]{0,3,2,1:T(8,128)(2,1)S(1)} %fusion.1), kind=kLoop, calls=%fused_computation | loop fusion | flops 4718592 | bytes 9437184 | tf_op jit(solution)/shard_map/stack | solution.py:95
  124.7 6.8 %copy.61 = bf16[2048,1152]{1,0:T(8,128)(2,1)} copy(bf16[2048,1152]{0,1:T(8,128)(2,1)} %bitcast.146) | data formatting | bytes 9437184
  131.5 3.3 %fusion.17 = bf16[64,4]{0,1:T(4,128)(2,1)S(1)} fusion(bf16[64,4,384]{2,0,1:T(8,128)(2,1)} %copy-done.4, bf16[1,2048,384]{2,1,0:T(8,128)(2,1)} %param.13, bf16[64,1,4,2048]{3,2,1,0:T(4,128)(2,1)} %all-to-all-done.1), kind=kOutput, calls=%fused_computation.27 | convolution fusion | flops 404225792 | bytes 2818560 | tf_op jit(solution)/shard_map/sjcf,jdf->sjcd/dot_general | solution.py:57
  134.8 0.1 copy.55
  135.0 1.7 fusion.7
  136.7 0.7 fusion.5
  137.4 0.1 pad_maximum_fusion.1
  137.5 0.9 copy.56
  138.4 34.8 %all_to_all.20 = bf16[64,1,4,2049]{3,2,1,0:T(4,128)(2,1)S(1)} all-to-all(bf16[64,1,4,2049]{3,2,1,0:T(4,128)(2,1)S(1)} %copy.56), channel_id=1, replica_groups=mesh['dp'=16,'expert'=64] {'expert'}, dimensions={0} | all-to-all | bytes 2098176 | tf_op jit(solution)/shard_map/all_to_all | solution.py:14
  173.2 1.6 split.8
  174.8 2.2 %reshape.152 = bf16[256,2048]{1,0:T(8,128)(2,1)} reshape(bf16[64,1,4,2048]{3,2,1,0:T(4,128)(2,1)} %split.8) | data formatting | bytes 2097152 | tf_op jit(solution)/shard_map/reshape | solution.py:82
  177.0 0.1 convert_reduce_fusion
  177.1 0.1 reshape.156
  177.2 0.1 select_reduce_fusion
  177.3 0.1 convert_element_type.125
  177.4 0.7 copy.57
  178.1 2.1 %convolution_convert_fusion.2 = bf16[16,2048]{1,0:T(8,128)(2,1)} fusion(pred[256,16]{0,1:T(8,128)(4,1)S(1)} %fusion.45, bf16[256,2048]{1,0:T(8,128)(2,1)} %reshape.152), kind=kOutput, calls=%fused_computation.15 | convolution fusion | flops 16809984 | bytes 1118208 | tf_op jit(solution)/shard_map/et,ed->td/dot_general | solution.py:84
  180.2 19.5 %reduce-scatter.4.cloned.1.call-done = bf16[128,1152]{1,0:T(8,128)(2,1)} async-done(((bf16[2048,1152]{1,0:T(8,128)(2,1)}), bf16[128,1152]{1,0:T(8,128)(2,1)}) %reduce-scatter.4.cloned.1.call-update) | async-done | bytes 294928
  199.7 1.2 copy.62
  201.0 0.8 copy.58
  201.8 0.8 copy.59
  202.6 0.8 copy.60
  (19 shorter events, 0.4 us)
Async XLA Ops:
  7.2 78.4 %copy-start = (bf16[1,2048,384]{2,1,0:T(8,128)(2,1)S(1)}, bf16[1,2048,384]{2,1,0:T(8,128)(2,1)}, u32[]{:S(2)}) copy-start(bf16[1,2048,384]{2,1,0:T(8,128)(2,1)} %param.11) | copy-start | bytes 4718596
  10.3 34.8 %all-to-all-start = ((bf16[64,1,4]{2,1,0:T(2,128)(2,1)}), bf16[64,1,4]{2,1,0:T(2,128)(2,1)S(1)}, u32[]{:S(2)}, u32[]{:S(2)}) async-start(bf16[64,1,4]{2,1,0:T(2,128)(2,1)} %convert_element_type.129), calls=%async_computation | async-start | bytes 65536 | tf_op jit(solution)/shard_map/all_to_all | solution.py:46
  37.0 13.6 %copy-start.3 = (bf16[16,2048]{1,0:T(8,128)(2,1)S(1)}, bf16[16,2048]{1,0:T(8,128)(2,1)}, u32[]{:S(2)}) copy-start(bf16[16,2048]{1,0:T(8,128)(2,1)} %param.8) | copy-start | bytes 196612
  45.1 31.3 %all-to-all-start.2 = ((bf16[64,1,4,2048]{3,2,1,0:T(4,128)(2,1)}), bf16[64,1,4,2048]{3,2,1,0:T(4,128)(2,1)}, u32[]{:S(2)}, u32[]{:S(2)}) async-start(bf16[64,1,4,2048]{3,2,1,0:T(4,128)(2,1)} %bitcast.8), calls=%async_computation.2 | async-start | bytes 2097152 | tf_op jit(solution)/shard_map/all_to_all | solution.py:44
  76.3 34.5 %all-to-all-start.1 = ((bf16[64,1,4,2048]{3,2,1,0:T(4,128)(2,1)}), bf16[64,1,4,2048]{3,2,1,0:T(4,128)(2,1)}, u32[]{:S(2)}, u32[]{:S(2)}) async-start(bf16[64,1,4,2048]{3,2,1,0:T(4,128)(2,1)} %bitcast.1), calls=%async_computation.1 | async-start | bytes 2097152 | tf_op jit(solution)/shard_map/all_to_all | solution.py:45
  85.2 114.5 %reduce-scatter.4.cloned.1.call-start = ((), (), s32[]{:S(2)}) async-start(), calls=%async_computation.5 | async-start | bytes 5013504
  85.6 3.1 %copy-start.1 = (bf16[1,2048,384]{2,1,0:T(8,128)(2,1)S(1)}, bf16[1,2048,384]{2,1,0:T(8,128)(2,1)}, u32[]{:S(2)}) copy-start(bf16[1,2048,384]{2,1,0:T(8,128)(2,1)} %param.12) | copy-start | bytes 4718596
  113.9 2.9 %copy-start.4 = (bf16[64,4,384]{2,0,1:T(8,128)(2,1)}, bf16[64,4,384]{2,0,1:T(8,128)(2,1)S(1)}, u32[]{:S(2)}) copy-start(bf16[64,4,384]{2,0,1:T(8,128)(2,1)S(1)} %get-tuple-element.27) | copy-start | bytes 589828
  113.9 5.6 %copy-start.2 = (bf16[64,1,4,384]{3,0,2,1:T(8,128)(2,1)}, bf16[64,1,4,384]{3,0,2,1:T(8,128)(2,1)S(1)}, u32[]{:S(2)}) copy-start(bf16[64,1,4,384]{3,0,2,1:T(8,128)(2,1)S(1)} %get-tuple-element.26) | copy-start | bytes 589828
Sparse Core Ops, SparseCore 0:
  131.6 68.0 reduce-scatter.3
where the time goes:
time: 211 us; the launch traced here: 210 us
  waiting for transfers between devices  70.8 us (34%)
  starting transfers between devices  38.5 us (18%)
  blocking collectives  34.8 us (16%)
  matrix products  27.1 us (13%)
  local copies, waits for them, and re-layouts  21.2 us (10%)
  between operations  14.3 us (7%)
  other arithmetic  3.57 us (2%)
    all_to_all x1, blocking collectives, side_by_side(): lax.all_to_all(both, axis, split_axis=split_dim, concat_axis=concat_dim,...  34.8 us
    all_to_all x1, waiting for transfers between devices, body(): lax.all_to_all(sent_x, 'expert', split_axis=0, concat_axis=0, tiled=True)  24 us
    all_to_all x1, starting transfers between devices, body(): lax.all_to_all(sent_p, 'expert', split_axis=0, concat_axis=0, tiled=True)  23.9 us
    unnamed x2, waiting for transfers between devices  19.5 us
    all_to_all x1, waiting for transfers between devices, body(): lax.all_to_all(sent_dy, 'expert', split_axis=0, concat_axis=0, tiled=True)  19.2 us
    unnamed x17, local copies, waits for them, and re-layouts  11.9 us
    all_to_all x1, starting transfers between devices, body(): lax.all_to_all(sent_dy, 'expert', split_axis=0, concat_axis=0, tiled=True)  8.86 us
    all_to_all x1, waiting for transfers between devices, body(): lax.all_to_all(sent_p, 'expert', split_axis=0, concat_axis=0, tiled=True)  8.03 us
  transfers between devices with their start and end apart: 4, of which 4 were waited for; matrix products, arithmetic and copies ran while one was open for 12% of the time, Pallas kernels for 0%

commit v1 on v0

v1 whole, which is shorter than its diff:
```python
import jax
import jax.numpy as jnp
from jax import lax
from jax.experimental import pallas as pl
from jax.experimental.pallas import tpu as pltpu
from jax.sharding import PartitionSpec as P

MESH = pl.DeviceIdType.MESH
F32, BF16 = jnp.float32, jnp.bfloat16
N = 8
OFF = (0, 1, 7, 2, 6, 3, 5, 4)
TOK, SLOT, D, FF, EXTRA = 16, 4, 2048, 384, 128
ROWS = N * N * SLOT
HALF = D // 2
GROUPS = 2
PER = N // GROUPS


def dot(a, b, ca=1, cb=0):
    return lax.dot_general(a, b, (((ca,), (cb,)), ((), ())), preferred_element_type=F32)


def iota(shape, axis):
    return lax.broadcasted_iota(jnp.int32, shape, axis)


def offset_of(k):
    return jnp.where(k % 2 == 1, (k + 1) // 2, (N - k // 2) % N)


def codes(weights):
    n = weights.shape[0]
    mask = weights.astype(F32) > 0.0
    r, c = iota((n, n), 0), iota((n, n), 1)
    before = jnp.where((r // TOK == c // TOK) & (c < r), 1.0, 0.0).astype(BF16)
    place = dot(before, jnp.where(mask, 1.0, 0.0).astype(BF16))
    return jnp.where(mask, place + 1.0, 0.0).astype(BF16)


def expert_lane(side, z, y, k):
    if side == 0:
        return z * N + (y + offset_of(k)) % N
    return ((z + offset_of(k)) % N) * N + y


def kernel(
    tok, dy, ids, pr, wg_h, wu_h, wd_h,
    tg_out, pg_out, gg_out, ug_out, dg_out,
    gather, send2, recv2, wgu, wd, gu, dyr, gbub, gbub_b, pact,
    contrib, back, tpart, trecv, part, other, ring_s, ring_r, ring1_s, ring1_r,
    wsem, p1s, p1r, p2s, p2r, c1s, c1r, c2s, c2r, ds, dr, rs, rr,
):
    dp, ex = lax.axis_index("dp"), lax.axis_index("expert")
    x, core = dp // 2, dp % 2
    z, y = ex // N, ex % N

    def along(side, d):
        if side == 0:
            return (dp, ((z + d) % N) * N + y)
        return (dp, z * N + (y + d) % N)

    ahead = (((x + 1) % N) * 2 + core, ex)
    behind = (((x + N - 1) % N) * 2 + core, ex)
    partner = (x * 2 + 1 - core, ex)

    loads = [
        pltpu.make_async_copy(wg_h.at[0], wgu.at[:, pl.ds(0, FF)], wsem.at[0]),
        pltpu.make_async_copy(wu_h.at[0], wgu.at[:, pl.ds(FF, FF)], wsem.at[1]),
        pltpu.make_async_copy(wd_h.at[0], wd, wsem.at[2]),
    ]
    for load in loads:
        load.start()

    barrier = pltpu.get_barrier_semaphore()
    peers = [along(side, d) for d in range(1, N) for side in range(2)] + [ahead, behind, partner]
    for peer in peers:
        pl.semaphore_signal(barrier, inc=1, device_id=peer, device_id_type=MESH)

    lane16 = iota((TOK, EXTRA), 1)
    dense = jnp.zeros((TOK, EXTRA), F32)
    for k in range(ids.shape[1]):
        dense += jnp.where(lane16 == ids[:, k : k + 1], pr[:, k : k + 1].astype(F32), 0.0)
    dense = dense.astype(BF16)
    for side, src in ((0, tok), (1, dy)):
        gather[side, 0:TOK, 0:D] = src[...]
        gather[side, 0:TOK, D : D + EXTRA] = dense

    pl.semaphore_wait(barrier, len(peers))

    sends = []

    def remote(src, dst, ssem, rsem, device):
        return pltpu.make_async_remote_copy(
            src_ref=src, dst_ref=dst, send_sem=ssem, recv_sem=rsem, device_id=device, device_id_type=MESH
        )

    def start(copy):
        copy.start()
        sends.append(copy)
        return copy

    hop1 = [[None] * N, [None] * N]
    for k in range(1, N):
        for side in range(2):
            hop1[side][k] = start(
                remote(
                    gather.at[side, pl.ds(0, TOK)], gather.at[side, pl.ds(TOK * k, TOK)],
                    p1s.at[side, k - 1], p1r.at[side, k - 1], along(side, OFF[k]),
                )
            )

    width = (D + EXTRA, D)
    hop2 = []
    for g in range(GROUPS):
        n_tok, n_row = PER * TOK, N * PER * SLOT
        for side in range(2):
            for k in range(max(1, g * PER), (g + 1) * PER):
                hop1[side][k].wait_recv()
            rows_at = pl.ds(g * n_tok, n_tok)
            code = codes(gather[side, rows_at, D : D + EXTRA])
            r, c = iota((n_row, EXTRA), 0), iota((n_row, EXTRA), 1)
            pick = jnp.where(c == expert_lane(side, z, y, r // (PER * SLOT)), 1.0, 0.0).astype(BF16)
            found = dot(pick, code, 1, 1)
            r, c = iota((n_row, n_tok), 0), iota((n_row, n_tok), 1)
            hit = (found == (r % SLOT + 1).astype(F32)) & ((r // SLOT) % PER == c // TOK)
            sel = jnp.where(hit, 1.0, 0.0).astype(BF16)

            def choose(cols, side=side, sel=sel, rows_at=rows_at, g=g):
                rows = dot(sel, gather[side, rows_at, cols]).astype(BF16)
                m = PER * SLOT
                for k in range(N):
                    target = send2 if k else recv2
                    target[side, pl.ds(k * N * SLOT + g * m, m), cols] = rows[k * m : (k + 1) * m]

            def tile(n, carry, choose=choose):
                choose(pl.ds(pl.multiple_of(n * 256, 256), 256))
                return carry

            lax.fori_loop(0, D // 256, tile, 0)
            if side == 0:
                choose(pl.ds(D, EXTRA))
            m = PER * SLOT
            for k in range(N - 1, 0, -1):
                at = pl.ds(k * N * SLOT + g * m, m)
                cols = pl.ds(0, width[side])
                hop2.append(
                    start(
                        remote(
                            send2.at[side, at, cols], recv2.at[side, at, cols],
                            p2s.at[side, g, k - 1], p2r.at[side, g, k - 1], along(1 - side, OFF[k]),
                        )
                    )
                )

    r, c = iota((ROWS, EXTRA), 0), iota((ROWS, EXTRA), 1)
    t, q = iota((N * TOK, ROWS), 0), iota((N * TOK, ROWS), 1)
    gives = []
    for side in range(2):
        code = codes(gather[side, :, D : D + EXTRA])
        pick = jnp.where(c == expert_lane(side, z, y, r // (N * SLOT)), 1.0, 0.0).astype(BF16)
        found = dot(code, pick, 1, 1)
        hit = (found == (q % SLOT + 1).astype(F32)) & ((q // SLOT) % N == t // TOK)
        gives.append(jnp.where(hit, 1.0, 0.0).astype(BF16))
    r, c = iota((ROWS, ROWS), 0), iota((ROWS, ROWS), 1)
    swapped = ((r // SLOT) % N) * (N * SLOT) + (r // (N * SLOT)) * SLOT + r % SLOT
    swap = jnp.where(c == swapped, 1.0, 0.0).astype(BF16)

    for load in loads:
        load.wait()
    for copy in hop2:
        copy.wait_recv()

    def tile_gu(n, carry):
        cols = pl.ds(pl.multiple_of(n * 256, 256), 256)
        gu[:, cols] = dot(recv2[0, :, 0:D], wgu[:, cols])
        return carry

    lax.fori_loop(0, 2 * FF // 256, tile_gu, 0)

    def tile_swap(n, carry):
        cols = pl.ds(pl.multiple_of(n * 256, 256), 256)
        dyr[:, cols] = dot(swap, recv2[1, :, cols]).astype(BF16)
        return carry

    lax.fori_loop(0, D // 256, tile_swap, 0)
    gu[:, 2 * FF : 3 * FF] = dot(dyr[...], wd[...])

    chunk = 32

    def middle(n, carry):
        at = pl.ds(pl.multiple_of(n * chunk, chunk), chunk)
        lane = iota((chunk, EXTRA), 1)
        p = jnp.sum(jnp.where(lane == ex, recv2[0, at, D : D + EXTRA].astype(F32), 0.0), axis=1, keepdims=True)
        gate, up, dyw = gu[at, 0:FF], gu[at, FF : 2 * FF], gu[at, 2 * FF : 3 * FF]
        sigma = 1.0 / (1.0 + jnp.exp(-gate))
        silu = gate * sigma
        act = (silu * up).astype(BF16).astype(F32)
        prob_back = jnp.sum(act * dyw, axis=1, keepdims=True)
        contrib[0, at, HALF : HALF + EXTRA] = jnp.where(lane == ex, prob_back, 0.0).astype(BF16)
        act_grad = p * dyw
        gbub[at, 0:FF] = (act_grad * up * sigma * (1.0 + gate * (1.0 - sigma))).astype(BF16)
        gbub[at, FF : 2 * FF] = (act_grad * silu).astype(BF16)
        pact[at, :] = (p * act).astype(BF16)
        return carry

    lax.fori_loop(0, ROWS // chunk, middle, 0)
    gbub_b[...] = dot(swap, gbub[...]).astype(BF16)

    line = N * SLOT
    widths = (HALF + EXTRA, HALF)
    back1 = []
    for side in range(2):
        mine = gbub if side == 0 else gbub_b

        def tile_c(n, carry, side=side, mine=mine):
            cols = pl.ds(pl.multiple_of(n * 256, 256), 256)
            w_rows = pl.ds(pl.multiple_of(side * HALF + n * 256, 256), 256)
            contrib[side, :, cols] = dot(mine[...], wgu[w_rows, :], 1, 1).astype(BF16)
            return carry

        lax.fori_loop(0, HALF // 256, tile_c, 0)
        cols = pl.ds(0, widths[side])
        for k in range(N - 1, 0, -1):
            at = pl.ds(k * line, line)
            back1.append(
                start(
                    remote(
                        contrib.at[side, at, cols], back.at[side, at, cols],
                        c1s.at[side, k - 1], c1r.at[side, k - 1], along(1 - side, N - OFF[k]),
                    )
                )
            )
        back[side, 0:line, cols] = contrib[side, 0:line, cols]

    def shards_gu(n, carry):
        cols = pl.ds(pl.multiple_of(((x + n) % N) * 256, 256), 256)
        both = dot(recv2[0, :, cols], gbub[...], 0, 0).astype(BF16)
        for m in range(2):
            for h in range(2):
                part[m, h, n] = both[h * 128 : h * 128 + 128, m * FF : (m + 1) * FF]
        return carry

    def shards_d(n, carry):
        cols = pl.ds(pl.multiple_of(((x + n) % N) * 256, 256), 256)
        both = dot(dyr[:, cols], pact[...], 0, 0).astype(BF16)
        for h in range(2):
            part[2, h, n] = both[h * 128 : h * 128 + 128]
        return carry

    swap_core = []

    def to_partner(m):
        swap_core.append(start(remote(part.at[m, 1 - core], other.at[m], ds.at[m], dr.at[m], partner)))

    lax.fori_loop(0, N, shards_gu, 0)
    to_partner(0)
    to_partner(1)
    lax.fori_loop(0, N, shards_d, 0)
    to_partner(2)

    def chip(m, rel, rows=pl.ds(0, 128)):
        return part[m, core, rel, rows, :].astype(F32) + other[m, rel, rows, :].astype(F32)

    towards = (ahead, behind)
    halves = (pl.ds(0, 64), pl.ds(64, 64))
    ring = {}
    for m in range(3):
        swap_core[m].wait_recv()
        for w in range(2):
            ring1_s[w, m] = chip(m, 4, halves[w]).astype(BF16)
            ring[w, 0, m] = start(
                remote(ring1_s.at[w, m], ring1_r.at[w, m], rs.at[w, 0, m], rr.at[w, 0, m], towards[w])
            )

    def ring_step(step):
        for m in range(3):
            for w in range(2):
                rel = 4 - step if w == 0 else 4 + step
                ring[w, step - 1, m].wait_recv()
                if step == 1:
                    a, b = halves[w], halves[1 - w]
                    ring_s[w, 0, m, a, :] = (chip(m, rel, a) + ring1_r[w, m].astype(F32)).astype(BF16)
                    ring_s[w, 0, m, b, :] = chip(m, rel, b).astype(BF16)
                else:
                    ring_s[w, step - 1, m] = (chip(m, rel) + ring_r[w, step - 2, m].astype(F32)).astype(BF16)
                ring[w, step, m] = start(
                    remote(
                        ring_s.at[w, step - 1, m], ring_r.at[w, step - 1, m],
                        rs.at[w, step, m], rr.at[w, step, m], towards[w],
                    )
                )

    ring_step(1)

    for copy in back1:
        copy.wait_recv()
    back_2 = []
    for side in range(2):
        for n in range(HALF // 256 + (side == 0)):
            size = 256 if n < HALF // 256 else EXTRA
            cols = pl.ds(n * 256, size)
            tpart[side, :, cols] = dot(gives[side], back[side, :, cols]).astype(BF16)
        cols = pl.ds(0, widths[side])
        for k in range(N - 1, 0, -1):
            at = pl.ds(k * TOK, TOK)
            back_2.append(
                start(
                    remote(
                        tpart.at[side, at, cols], trecv.at[side, at, cols],
                        c2s.at[side, k - 1], c2r.at[side, k - 1], along(side, N - OFF[k]),
                    )
                )
            )
        trecv[side, 0:TOK, cols] = tpart[side, 0:TOK, cols]

    ring_step(2)
    ring_step(3)

    for copy in back_2:
        copy.wait_recv()
    for side in range(2):
        total = jnp.zeros((TOK, HALF), F32)
        for k in range(N):
            total += trecv[side, k * TOK : (k + 1) * TOK, 0:HALF].astype(F32)
        tg_out[:, side * HALF : (side + 1) * HALF] = total.astype(BF16)
    dense = jnp.zeros((TOK, EXTRA), F32)
    for k in range(N):
        dense += trecv[0, k * TOK : (k + 1) * TOK, HALF : HALF + EXTRA].astype(F32)
    for k in range(ids.shape[1]):
        one = jnp.sum(jnp.where(lane16 == ids[:, k : k + 1], dense, 0.0), axis=1, keepdims=True)
        pg_out[:, k : k + 1] = one.astype(BF16)

    for m, out in enumerate((gg_out, ug_out, dg_out)):
        ring[0, 3, m].wait_recv()
        ring[1, 3, m].wait_recv()
        out[0] = chip(m, 0) + ring_r[0, 2, m].astype(F32) + ring_r[1, 2, m].astype(F32)

    for copy in sends:
        copy.wait_send()


def body(tokens, out_grad, expert_ids, probs, w_gate, w_up, w_down):
    vmem = pl.BlockSpec(memory_space=pltpu.VMEM)
    hbm = pl.BlockSpec(memory_space=pl.ANY)
    grads = jax.ShapeDtypeStruct((1, 128, FF), F32)
    dma = pltpu.SemaphoreType.DMA
    return pl.pallas_call(
        kernel,
        out_shape=(
            jax.ShapeDtypeStruct(tokens.shape, BF16),
            jax.ShapeDtypeStruct(probs.shape, BF16),
            grads, grads, grads,
        ),
        in_specs=[vmem] * 4 + [hbm] * 3,
        out_specs=(vmem,) * 5,
        scratch_shapes=[
            pltpu.VMEM((2, N * TOK, D + EXTRA), BF16),
            pltpu.VMEM((2, ROWS, D + EXTRA), BF16),
            pltpu.VMEM((2, ROWS, D + EXTRA), BF16),
            pltpu.VMEM((D, 2 * FF), BF16),
            pltpu.VMEM((D, FF), BF16),
            pltpu.VMEM((ROWS, 3 * FF), F32),
            pltpu.VMEM((ROWS, D), BF16),
            pltpu.VMEM((ROWS, 2 * FF), BF16),
            pltpu.VMEM((ROWS, 2 * FF), BF16),
            pltpu.VMEM((ROWS, FF), BF16),
            pltpu.VMEM((2, ROWS, HALF + EXTRA), BF16),
            pltpu.VMEM((2, ROWS, HALF + EXTRA), BF16),
            pltpu.VMEM((2, N * TOK, HALF + EXTRA), BF16),
            pltpu.VMEM((2, N * TOK, HALF + EXTRA), BF16),
            pltpu.VMEM((3, 2, N, 128, FF), BF16),
            pltpu.VMEM((3, N, 128, FF), BF16),
            pltpu.VMEM((2, 3, 3, 128, FF), BF16),
            pltpu.VMEM((2, 3, 3, 128, FF), BF16),
            pltpu.VMEM((2, 3, 64, FF), BF16),
            pltpu.VMEM((2, 3, 64, FF), BF16),
            dma((3,)),
            dma((2, N - 1)), dma((2, N - 1)),
            dma((2, GROUPS, N - 1)), dma((2, GROUPS, N - 1)),
            dma((2, N - 1)), dma((2, N - 1)),
            dma((2, N - 1)), dma((2, N - 1)),
            dma((3,)), dma((3,)),
            dma((2, 4, 3)), dma((2, 4, 3)),
        ],
        compiler_params=pltpu.CompilerParams(collective_id=0, has_side_effects=True),
        name="expert_layer_backward",
    )(tokens, out_grad, expert_ids, probs, w_gate, w_up, w_down)


def solution(mesh):
    rows = P(("dp", "expert"), None)
    weights = P("expert", None, None)
    grads = P("expert", "dp", None)
    return jax.shard_map(
        body,
        mesh=mesh,
        in_specs=(rows, rows, rows, rows, weights, weights, weights),
        out_specs=(rows, rows, grads, grads, grads),
        check_vma=False,
    )
```

time: 211 us -> 111 us (0.53)
  Pallas kernels: 0 us -> 99.3 us
  waiting for transfers between devices: 70.8 us -> 0 us
  starting transfers between devices: 38.5 us -> 0 us
  blocking collectives: 34.8 us -> 0 us
  matrix products: 27.1 us -> 0 us
  between operations: 14.3 us -> 0.64 us
  local copies, waits for them, and re-layouts: 21.2 us -> 10.3 us
  other arithmetic: 3.57 us -> 0 us
    pallas_call x0 -> x1, Pallas kernels: none -> 99.3 us  [body(): pl.pallas_call(kernel, out_shape=(jax.ShapeDtypeStruct(tokens.shape, BF16...]
    all_to_all x3 -> x0, waiting for transfers between devices: 51.3 us -> none  [the longest x1 24 us: body(): lax.all_to_all(sent_x, 'expert', split_axis=0, concat_axis=0, tiled=True)]
    all_to_all x3 -> x0, starting transfers between devices: 38.3 us -> none  [the longest x1 23.9 us: body(): lax.all_to_all(sent_p, 'expert', split_axis=0, concat_axis=0, tiled=True)]
    all_to_all x1 -> x0, blocking collectives: 34.8 us -> none  [side_by_side(): lax.all_to_all(both, axis, split_axis=split_dim, concat_axis=concat_dim,...]
    dot_general x12 -> x0, matrix products: 27.1 us -> none  [the longest x1 3.35 us: body(): jnp.einsum('sjcf,jdf->sjcd', expert_act, w_down, preferred_element_type=j...]
    unnamed x2 -> x0, waiting for transfers between devices: 19.5 us -> none
    reshape x3 -> x0, local copies, waits for them, and re-layouts: 4.64 us -> none  [the longest x1 2.16 us: body(): back_rows = back_rows.reshape(experts * slots, width)]
    unnamed x17 -> x6, local copies, waits for them, and re-layouts: 11.9 us -> 9.02 us
  transfers between devices with their start and end apart: 4 -> 0, of which waited for: 4 -> 0; matrix products, arithmetic and copies ran while one was open for 12% -> 0% of each run, Pallas kernels for 0% -> 0%
where the time goes in v1:
time: 111 us; the launch traced here: 110 us
  Pallas kernels  99.3 us (89%)
  local copies, waits for them, and re-layouts  10.3 us (9%)
    pallas_call x1, Pallas kernels, body(): pl.pallas_call(kernel, out_shape=(jax.ShapeDtypeStruct(tokens.shape, BF16...  99.3 us
    unnamed x6, local copies, waits for them, and re-layouts  9.02 us

profile of v1, /device:TPU:1, one launch (start us, length us, event | category | flops | bytes accessed | tf_op | source)
XLA Modules:
  0.0 110.3 jit_solution(18048948950724414728)
XLA Ops:
  0.6 1.3 %copy.13.pr = bf16[16,8]{1,0:T(8,128)(2,1)} copy(bf16[16,8]{0,1:T(8,128)(2,1)} %param.10) | data formatting | bytes 512 | tf_op args[3]
  2.0 1.4 %copy.12.ids = s32[16,8]{1,0:T(8,128)} copy(s32[16,8]{0,1:T(8,128)} %param.9) | data formatting | bytes 1024 | tf_op args[2]
  3.3 99.3 %expert_layer_backward.1 = (bf16[16,2048]{1,0:T(8,128)(2,1)}, bf16[16,8]{1,0:T(8,128)(2,1)}, f32[1,128,384]{2,1,0:T(8,128)}, f32[1,128,384]{2,1,0:T(8,128)}, f32[1,128,384]{2,1,0:T(8,128)}) custom-call(bf16[16,2048]{1,0:T(8,128)(2,1)} %tok.1, bf16[16,2048]{1,0:T(8,128)(2,1)} %dy.1, s32[16,8]{1,0:T(8,128)} %copy.12.ids, bf16[16,8]{1,0:T(8,128)(2,1)} %copy.13.pr, ...), custom_call_target="tpu_custom_call" | custom-call | tf_op jit(solution)/shard_map/expert_layer_backward/pallas_call | solution.py:347
  102.7 1.3 %copy.14 = bf16[16,8]{0,1:T(8,128)(2,1)} copy(bf16[16,8]{1,0:T(8,128)(2,1)} %get-tuple-element.6) | data formatting | bytes 512 | tf_op jit(solution)/shard_map/expert_layer_backward/pallas_call | solution.py:347
  104.0 1.5 %copy.19 = bf16[16,2048]{1,0:T(8,128)(2,1)} copy(bf16[16,2048]{1,0:T(8,128)(2,1)} %get-tuple-element.15) | data formatting | bytes 131072
  105.5 1.6 %copy.20 = f32[1,128,384]{2,1,0:T(8,128)} copy(f32[1,128,384]{2,1,0:T(8,128)} %get-tuple-element.17) | data formatting | bytes 393216
  107.1 1.6 %copy.21 = f32[1,128,384]{2,1,0:T(8,128)} copy(f32[1,128,384]{2,1,0:T(8,128)} %get-tuple-element.18) | data formatting | bytes 393216
  108.7 1.6 %copy.22 = f32[1,128,384]{2,1,0:T(8,128)} copy(f32[1,128,384]{2,1,0:T(8,128)} %get-tuple-element.19) | data formatting | bytes 393216

commit v2 on v1

--- a/solution.py
+++ b/solution.py
@@ -13,6 +13,7 @@
 ROWS = N * N * SLOT
 HALF = D // 2
 GROUPS = 2
+VMEM_LIMIT = 209 << 18
 PER = N // GROUPS
 
 
@@ -45,7 +46,7 @@
 
 def kernel(
     tok, dy, ids, pr, wg_h, wu_h, wd_h,
-    tg_out, pg_out, gg_out, ug_out, dg_out,
+    tg_out, pg_out, grads_out,
     gather, send2, recv2, wgu, wd, gu, dyr, gbub, gbub_b, pact,
     contrib, back, tpart, trecv, part, other, ring_s, ring_r, ring1_s, ring1_r,
     wsem, p1s, p1r, p2s, p2r, c1s, c1r, c2s, c2r, ds, dr, rs, rr,
@@ -76,11 +77,13 @@
     for peer in peers:
         pl.semaphore_signal(barrier, inc=1, device_id=peer, device_id_type=MESH)
 
-    lane16 = iota((TOK, EXTRA), 1)
-    dense = jnp.zeros((TOK, EXTRA), F32)
-    for k in range(ids.shape[1]):
-        dense += jnp.where(lane16 == ids[:, k : k + 1], pr[:, k : k + 1].astype(F32), 0.0)
-    dense = dense.astype(BF16)
+    top = ids.shape[0]
+    wide = pr[...].astype(F32)
+    expert = iota((EXTRA, TOK), 0)
+    dense = jnp.zeros((EXTRA, TOK), F32)
+    for k in range(top):
+        dense += jnp.where(expert == ids[k : k + 1, :], wide[k : k + 1, :], 0.0)
+    dense = dense.T.astype(BF16)
     for side, src in ((0, tok), (1, dy)):
         gather[side, 0:TOK, 0:D] = src[...]
         gather[side, 0:TOK, D : D + EXTRA] = dense
@@ -99,23 +102,32 @@
         sends.append(copy)
         return copy
 
-    hop1 = [[None] * N, [None] * N]
-    for k in range(1, N):
+    def share(side, i, src_slab, dst_slab, d, cols):
+        src, dst = (gather.at[side, pl.ds(TOK * k, TOK), cols] for k in (src_slab, dst_slab))
+        return start(remote(src, dst, p1s.at[side, i], p1r.at[side, i], along(side, d % N)))
+
+    every = pl.ds(0, D + EXTRA)
+    first, second = pl.ds(0, HALF), pl.ds(HALF, HALF + EXTRA)
+    hop1 = [[[] for _ in range(N)] for _ in range(2)]
+    for k in (3, 4, 1, 2):
         for side in range(2):
-            hop1[side][k] = start(
-                remote(
-                    gather.at[side, pl.ds(0, TOK)], gather.at[side, pl.ds(TOK * k, TOK)],
-                    p1s.at[side, k - 1], p1r.at[side, k - 1], along(side, OFF[k]),
-                )
-            )
+            hop1[side][k].append(share(side, k - 1, 0, k, OFF[k], every))
+    for slab, to, d, i, cols in ((3, 5, 1, 6, first), (4, 6, -1, 7, second)):
+        for side in range(2):
+            for copy in hop1[side][slab]:
+                copy.wait_recv()
+            hop1[side][slab] = []
+            hop1[side][to].append(share(side, to - 1, slab, to, d, every))
+            hop1[side][N - 1].append(share(side, i, slab, N - 1, 2 * d, cols))
 
     width = (D + EXTRA, D)
     hop2 = []
     for g in range(GROUPS):
         n_tok, n_row = PER * TOK, N * PER * SLOT
         for side in range(2):
-            for k in range(max(1, g * PER), (g + 1) * PER):
-                hop1[side][k].wait_recv()
+            for k in range(g * PER, (g + 1) * PER):
+                for copy in hop1[side][k]:
+                    copy.wait_recv()
             rows_at = pl.ds(g * n_tok, n_tok)
             code = codes(gather[side, rows_at, D : D + EXTRA])
             r, c = iota((n_row, EXTRA), 0), iota((n_row, EXTRA), 1)
@@ -206,6 +218,39 @@
     lax.fori_loop(0, ROWS // chunk, middle, 0)
     gbub_b[...] = dot(swap, gbub[...]).astype(BF16)
 
+    swap_core = {}
+
+    def shards(n):
+        cols = pl.ds(pl.multiple_of(((x + n) % N) * 256, 256), 256)
+        both = dot(recv2[0, :, cols], gbub[...], 0, 0).astype(BF16)
+        down = dot(dyr[:, cols], pact[...], 0, 0).astype(BF16)
+        for h in range(2):
+            rows = slice(h * 128, h * 128 + 128)
+            part[n, h, 0] = both[rows, 0:FF]
+            part[n, h, 1] = both[rows, FF : 2 * FF]
+            part[n, h, 2] = down[rows]
+        swap_core[n] = start(remote(part.at[n, 1 - core], other.at[n], ds.at[n], dr.at[n], partner))
+
+    def chip(m, rel, rows=pl.ds(0, 128)):
+        return part[rel, core, m, rows, :].astype(F32) + other[rel, m, rows, :].astype(F32)
+
+    for n in (4, 3, 5):
+        shards(n)
+
+    towards = (ahead, behind)
+    halves = (pl.ds(0, 64), pl.ds(64, 64))
+    ring = {}
+    swap_core[4].wait_recv()
+    for m in range(3):
+        for w in range(2):
+            ring1_s[w, m] = chip(m, 4, halves[w]).astype(BF16)
+            ring[w, 0, m] = start(
+                remote(ring1_s.at[w, m], ring1_r.at[w, m], rs.at[w, 0, m], rr.at[w, 0, m], towards[w])
+            )
+
+    for n in (2, 6, 1, 7, 0):
+        shards(n)
+
     line = N * SLOT
     widths = (HALF + EXTRA, HALF)
     back1 = []
@@ -232,47 +277,9 @@
             )
         back[side, 0:line, cols] = contrib[side, 0:line, cols]
 
-    def shards_gu(n, carry):
-        cols = pl.ds(pl.multiple_of(((x + n) % N) * 256, 256), 256)
-        both = dot(recv2[0, :, cols], gbub[...], 0, 0).astype(BF16)
-        for m in range(2):
-            for h in range(2):
-                part[m, h, n] = both[h * 128 : h * 128 + 128, m * FF : (m + 1) * FF]
-        return carry
-
-    def shards_d(n, carry):
-        cols = pl.ds(pl.multiple_of(((x + n) % N) * 256, 256), 256)
-        both = dot(dyr[:, cols], pact[...], 0, 0).astype(BF16)
-        for h in range(2):
-            part[2, h, n] = both[h * 128 : h * 128 + 128]
-        return carry
-
-    swap_core = []
-
-    def to_partner(m):
-        swap_core.append(start(remote(part.at[m, 1 - core], other.at[m], ds.at[m], dr.at[m], partner)))
-
-    lax.fori_loop(0, N, shards_gu, 0)
-    to_partner(0)
-    to_partner(1)
-    lax.fori_loop(0, N, shards_d, 0)
-    to_partner(2)
-
-    def chip(m, rel, rows=pl.ds(0, 128)):
-        return part[m, core, rel, rows, :].astype(F32) + other[m, rel, rows, :].astype(F32)
-
-    towards = (ahead, behind)
-    halves = (pl.ds(0, 64), pl.ds(64, 64))
-    ring = {}
-    for m in range(3):
-        swap_core[m].wait_recv()
-        for w in range(2):
-            ring1_s[w, m] = chip(m, 4, halves[w]).astype(BF16)
-            ring[w, 0, m] = start(
-                remote(ring1_s.at[w, m], ring1_r.at[w, m], rs.at[w, 0, m], rr.at[w, 0, m], towards[w])
-            )
-
     def ring_step(step):
+        swap_core[4 - step].wait_recv()
+        swap_core[4 + step].wait_recv()
         for m in range(3):
             for w in range(2):
                 rel = 4 - step if w == 0 else 4 + step
@@ -291,6 +298,7 @@
                 )
 
     ring_step(1)
+    ring_step(2)
 
     for copy in back1:
         copy.wait_recv()
@@ -313,7 +321,6 @@
             )
         trecv[side, 0:TOK, cols] = tpart[side, 0:TOK, cols]
 
-    ring_step(2)
     ring_step(3)
 
     for copy in back_2:
@@ -326,33 +333,40 @@
     dense = jnp.zeros((TOK, EXTRA), F32)
     for k in range(N):
         dense += trecv[0, k * TOK : (k + 1) * TOK, HALF : HALF + EXTRA].astype(F32)
-    for k in range(ids.shape[1]):
-        one = jnp.sum(jnp.where(lane16 == ids[:, k : k + 1], dense, 0.0), axis=1, keepdims=True)
-        pg_out[:, k : k + 1] = one.astype(BF16)
-
-    for m, out in enumerate((gg_out, ug_out, dg_out)):
+    dense = dense.T
+    for k in range(top):
+        one = jnp.where(expert == ids[k : k + 1, :], dense, 0.0)
+        pg_out[k : k + 1, :] = jnp.sum(one, axis=0, keepdims=True)
+
+    swap_core[0].wait_recv()
+    for m in range(3):
         ring[0, 3, m].wait_recv()
         ring[1, 3, m].wait_recv()
-        out[0] = chip(m, 0) + ring_r[0, 2, m].astype(F32) + ring_r[1, 2, m].astype(F32)
+        grads_out[m] = chip(m, 0) + ring_r[0, 2, m].astype(F32) + ring_r[1, 2, m].astype(F32)
 
     for copy in sends:
         copy.wait_send()
 
 
+def finish(tg, pg, grads, tg_out, pg_out, gg_out, ug_out, dg_out):
+    tg_out[...] = tg[...]
+    pg_out[...] = pg[...].astype(BF16)
+    for m, out in enumerate((gg_out, ug_out, dg_out)):
+        out[0] = grads[m]
+
+
 def body(tokens, out_grad, expert_ids, probs, w_gate, w_up, w_down):
     vmem = pl.BlockSpec(memory_space=pltpu.VMEM)
-    hbm = pl.BlockSpec(memory_space=pl.ANY)
+    hbm = pl.BlockSpec(memory_space=pltpu.HBM)
     grads = jax.ShapeDtypeStruct((1, 128, FF), F32)
+    token_grad = jax.ShapeDtypeStruct(tokens.shape, BF16)
+    small = probs.T.shape
     dma = pltpu.SemaphoreType.DMA
-    return pl.pallas_call(
+    sums = pl.pallas_call(
         kernel,
-        out_shape=(
-            jax.ShapeDtypeStruct(tokens.shape, BF16),
-            jax.ShapeDtypeStruct(probs.shape, BF16),
-            grads, grads, grads,
-        ),
+        out_shape=(token_grad, jax.ShapeDtypeStruct(small, F32), jax.ShapeDtypeStruct((3, 128, FF), F32)),
         in_specs=[vmem] * 4 + [hbm] * 3,
-        out_specs=(vmem,) * 5,
+        out_specs=(vmem,) * 3,
         scratch_shapes=[
             pltpu.VMEM((2, N * TOK, D + EXTRA), BF16),
             pltpu.VMEM((2, ROWS, D + EXTRA), BF16),
@@ -368,23 +382,32 @@
             pltpu.VMEM((2, ROWS, HALF + EXTRA), BF16),
             pltpu.VMEM((2, N * TOK, HALF + EXTRA), BF16),
             pltpu.VMEM((2, N * TOK, HALF + EXTRA), BF16),
-            pltpu.VMEM((3, 2, N, 128, FF), BF16),
-            pltpu.VMEM((3, N, 128, FF), BF16),
+            pltpu.VMEM((N, 2, 3, 128, FF), BF16),
+            pltpu.VMEM((N, 3, 128, FF), BF16),
             pltpu.VMEM((2, 3, 3, 128, FF), BF16),
             pltpu.VMEM((2, 3, 3, 128, FF), BF16),
             pltpu.VMEM((2, 3, 64, FF), BF16),
             pltpu.VMEM((2, 3, 64, FF), BF16),
             dma((3,)),
-            dma((2, N - 1)), dma((2, N - 1)),
+            dma((2, N)), dma((2, N)),
             dma((2, GROUPS, N - 1)), dma((2, GROUPS, N - 1)),
             dma((2, N - 1)), dma((2, N - 1)),
             dma((2, N - 1)), dma((2, N - 1)),
-            dma((3,)), dma((3,)),
+            dma((N,)), dma((N,)),
             dma((2, 4, 3)), dma((2, 4, 3)),
         ],
-        compiler_params=pltpu.CompilerParams(collective_id=0, has_side_effects=True),
+        compiler_params=pltpu.CompilerParams(collective_id=0, has_side_effects=True, vmem_limit_bytes=VMEM_LIMIT),
         name="expert_layer_backward",
-    )(tokens, out_grad, expert_ids, probs, w_gate, w_up, w_down)
+    )(tokens, out_grad, expert_ids.T, probs.T, w_gate, w_up, w_down)
+    token_grad, prob_grad, *weight_grads = pl.pallas_call(
+        finish,
+        out_shape=(token_grad, jax.ShapeDtypeStruct(small, BF16), grads, grads, grads),
+        in_specs=[vmem] * 3,
+        out_specs=(vmem,) * 5,
+        compiler_params=pltpu.CompilerParams(vmem_limit_bytes=4 << 20),
+        name="write_outputs",
+    )(*sums)
+    return (token_grad, prob_grad.T, *weight_grads)
 
 
 def solution(mesh):

time: 111 us -> 97.2 us (0.88)
  local copies, waits for them, and re-layouts: 10.3 us -> 3.04 us
  Pallas kernels: 99.3 us -> 93.2 us
    pallas_call x1 -> x2, Pallas kernels: 99.3 us -> 93.2 us  [the longest x1 92.3 us: body(): pl.pallas_call(kernel, out_shape=(token_grad, jax.ShapeDtypeStruct(small,...]
    unnamed x6 -> x8, local copies, waits for them, and re-layouts: 9.02 us -> 3.04 us
    pallas_call x1 -> x0, local copies, waits for them, and re-layouts: 1.33 us -> none  [body(): pl.pallas_call(kernel, out_shape=(jax.ShapeDtypeStruct(tokens.shape, BF16...]
where the time goes in v2:
time: 97.2 us; the launch traced here: 96.9 us
  Pallas kernels  93.2 us (96%)
  local copies, waits for them, and re-layouts  3.04 us (3%)
    pallas_call x1, Pallas kernels, body(): pl.pallas_call(kernel, out_shape=(token_grad, jax.ShapeDtypeStruct(small,...  92.3 us
    unnamed x8, local copies, waits for them, and re-layouts  3.04 us

profile of v2, /device:TPU:1, one launch (start us, length us, event | category | flops | bytes accessed | tf_op | source)
XLA Modules:
  0.0 96.9 jit_solution(14794601995454386991)
XLA Ops:
  0.6 0.0 copy-start
  0.6 0.8 copy-done
  1.5 0.0 copy-start.1
  1.5 0.8 copy-done.1
  2.3 0.0 copy-start.2
  2.3 0.7 copy-done.2
  3.0 0.0 copy-start.3
  3.0 0.7 copy-done.3
  3.7 92.3 %expert_layer_backward.1 = (bf16[16,2048]{1,0:T(8,128)(2,1)S(1)}, f32[8,16]{1,0:T(8,128)S(1)}, f32[3,128,384]{2,1,0:T(8,128)S(1)}) custom-call(bf16[16,2048]{1,0:T(8,128)(2,1)S(1)} %copy-done, bf16[16,2048]{1,0:T(8,128)(2,1)S(1)} %copy-done.1, s32[8,16]{1,0:T(8,128)S(1)} %bitcast.3, bf16[8,16]{1,0:T(8,128)(2,1)S(1)} %bitcast.4, bf16[1,2048,384]{2,1,0:T(8,128)(2,1)} %wg_h.1, ...), custom_call_target="tpu_custom_call" | custom-call | tf_op jit(solution)/shard_map/expert_layer_backward/pallas_call | solution.py:365
  96.0 0.9 write_outputs.1
Async XLA Ops:
  0.6 0.8 copy-start
  1.5 0.8 copy-start.1
  2.3 0.7 copy-start.2
  3.0 0.7 copy-start.3

commit v3 on v2

--- a/solution.py
+++ b/solution.py
@@ -45,11 +45,11 @@
 
 
 def kernel(
-    tok, dy, ids, pr, wg_h, wu_h, wd_h,
+    tok_h, dy_h, ids_h, pr_h, wg_h, wu_h, wd_h,
     tg_out, pg_out, grads_out,
-    gather, send2, recv2, wgu, wd, gu, dyr, gbub, gbub_b, pact,
+    ids, pr, gather, send2, recv2, wgu, wd, gu, dyr, gbub, gbub_b, pact,
     contrib, back, tpart, trecv, part, other, ring_s, ring_r, ring1_s, ring1_r,
-    wsem, p1s, p1r, p2s, p2r, c1s, c1r, c2s, c2r, ds, dr, rs, rr,
+    isem, wsem, p1s, p1r, p2s, p2r, c1s, c1r, c2s, c2r, ds, dr, rs, rr,
 ):
     dp, ex = lax.axis_index("dp"), lax.axis_index("expert")
     x, core = dp // 2, dp % 2
@@ -64,6 +64,15 @@
     behind = (((x + N - 1) % N) * 2 + core, ex)
     partner = (x * 2 + 1 - core, ex)
 
+    inputs = [
+        pltpu.make_async_copy(src, dst, isem.at[i])
+        for i, (src, dst) in enumerate((
+            (ids_h, ids), (pr_h, pr),
+            (tok_h, gather.at[0, pl.ds(0, TOK), pl.ds(0, D)]), (dy_h, gather.at[1, pl.ds(0, TOK), pl.ds(0, D)]),
+        ))
+    ]
+    for load in inputs:
+        load.start()
     loads = [
         pltpu.make_async_copy(wg_h.at[0], wgu.at[:, pl.ds(0, FF)], wsem.at[0]),
         pltpu.make_async_copy(wu_h.at[0], wgu.at[:, pl.ds(FF, FF)], wsem.at[1]),
@@ -77,6 +86,8 @@
     for peer in peers:
         pl.semaphore_signal(barrier, inc=1, device_id=peer, device_id_type=MESH)
 
+    for load in inputs:
+        load.wait()
     top = ids.shape[0]
     wide = pr[...].astype(F32)
     expert = iota((EXTRA, TOK), 0)
@@ -84,8 +95,7 @@
     for k in range(top):
         dense += jnp.where(expert == ids[k : k + 1, :], wide[k : k + 1, :], 0.0)
     dense = dense.T.astype(BF16)
-    for side, src in ((0, tok), (1, dy)):
-        gather[side, 0:TOK, 0:D] = src[...]
+    for side in range(2):
         gather[side, 0:TOK, D : D + EXTRA] = dense
 
     pl.semaphore_wait(barrier, len(peers))
@@ -362,12 +372,16 @@
     token_grad = jax.ShapeDtypeStruct(tokens.shape, BF16)
     small = probs.T.shape
     dma = pltpu.SemaphoreType.DMA
+    held = (tokens, out_grad, expert_ids.T, probs.T, w_gate, w_up, w_down)
+    stay = [pltpu.with_memory_space_constraint(a, pltpu.HBM) for a in held]
     sums = pl.pallas_call(
         kernel,
         out_shape=(token_grad, jax.ShapeDtypeStruct(small, F32), jax.ShapeDtypeStruct((3, 128, FF), F32)),
-        in_specs=[vmem] * 4 + [hbm] * 3,
+        in_specs=[hbm] * 7,
         out_specs=(vmem,) * 3,
         scratch_shapes=[
+            pltpu.VMEM(small, jnp.int32),
+            pltpu.VMEM(small, BF16),
             pltpu.VMEM((2, N * TOK, D + EXTRA), BF16),
             pltpu.VMEM((2, ROWS, D + EXTRA), BF16),
             pltpu.VMEM((2, ROWS, D + EXTRA), BF16),
@@ -388,6 +402,7 @@
             pltpu.VMEM((2, 3, 3, 128, FF), BF16),
             pltpu.VMEM((2, 3, 64, FF), BF16),
             pltpu.VMEM((2, 3, 64, FF), BF16),
+            dma((4,)),
             dma((3,)),
             dma((2, N)), dma((2, N)),
             dma((2, GROUPS, N - 1)), dma((2, GROUPS, N - 1)),
@@ -398,7 +413,7 @@
         ],
         compiler_params=pltpu.CompilerParams(collective_id=0, has_side_effects=True, vmem_limit_bytes=VMEM_LIMIT),
         name="expert_layer_backward",
-    )(tokens, out_grad, expert_ids.T, probs.T, w_gate, w_up, w_down)
+    )(*stay)
     token_grad, prob_grad, *weight_grads = pl.pallas_call(
         finish,
         out_shape=(token_grad, jax.ShapeDtypeStruct(small, BF16), grads, grads, grads),

time: 97.2 us -> 94.1 us (0.968)
  local copies, waits for them, and re-layouts: 3.04 us -> 0 us
    unnamed x8 -> x0, local copies, waits for them, and re-layouts: 3.04 us -> none
where the time goes in v3:
time: 94.1 us; the launch traced here: 93.9 us
  Pallas kernels  93.3 us (99%)
    pallas_call x1, Pallas kernels, body(): pl.pallas_call(kernel, out_shape=(token_grad, jax.ShapeDtypeStruct(small,...  92.4 us

profile of v3, /device:TPU:1, one launch (start us, length us, event | category | flops | bytes accessed | tf_op | source)
XLA Modules:
  0.0 93.9 jit_solution(11215031591209844556)
XLA Ops:
  0.6 92.4 %expert_layer_backward.1 = (bf16[16,2048]{1,0:T(8,128)(2,1)S(1)}, f32[8,16]{1,0:T(8,128)S(1)}, f32[3,128,384]{2,1,0:T(8,128)S(1)}) custom-call(bf16[16,2048]{1,0:T(8,128)(2,1)} %tok_h.1, bf16[16,2048]{1,0:T(8,128)(2,1)} %dy_h.1, s32[8,16]{1,0:T(8,128)} %bitcast.3, bf16[8,16]{1,0:T(8,128)(2,1)} %bitcast.4, bf16[1,2048,384]{2,1,0:T(8,128)(2,1)} %wg_h.1, ...), custom_call_target="tpu_custom_call" | custom-call | tf_op jit(solution)/shard_map/expert_layer_backward/pallas_call | solution.py:377
  93.0 0.9 write_outputs.1

commit v4 on v3

--- a/solution.py
+++ b/solution.py
@@ -15,6 +15,7 @@
 GROUPS = 2
 VMEM_LIMIT = 209 << 18
 PER = N // GROUPS
+CHUNKS = 2
 
 
 def dot(a, b, ca=1, cb=0):
@@ -226,7 +227,6 @@
         return carry
 
     lax.fori_loop(0, ROWS // chunk, middle, 0)
-    gbub_b[...] = dot(swap, gbub[...]).astype(BF16)
 
     swap_core = {}
 
@@ -244,8 +244,54 @@
     def chip(m, rel, rows=pl.ds(0, 128)):
         return part[rel, core, m, rows, :].astype(F32) + other[rel, m, rows, :].astype(F32)
 
-    for n in (4, 3, 5):
-        shards(n)
+    line, wide_cols = N * SLOT, HALF // CHUNKS
+
+    def chunk_cols(side, ch):
+        last = EXTRA if side == 0 and ch == CHUNKS - 1 else 0
+        return pl.ds(ch * wide_cols, wide_cols + last)
+
+    back1 = {}
+
+    def send_back(side, ch):
+        mine = gbub if side == 0 else gbub_b
+        for n in range(wide_cols // 256):
+            at = ch * wide_cols + n * 256
+            weights = wgu[side * HALF + at : side * HALF + at + 256, :]
+            contrib[side, :, at : at + 256] = dot(mine[...], weights, 1, 1).astype(BF16)
+        cols = chunk_cols(side, ch)
+        for k in range(N - 1, 0, -1):
+            at = pl.ds(k * line, line)
+            back1[side, ch, k] = start(
+                remote(
+                    contrib.at[side, at, cols], back.at[side, at, cols],
+                    c1s.at[side, ch, k - 1], c1r.at[side, ch, k - 1], along(1 - side, N - OFF[k]),
+                )
+            )
+        back[side, 0:line, cols] = contrib[side, 0:line, cols]
+
+    back2 = []
+
+    def send_home(side, ch):
+        for k in range(1, N):
+            back1[side, ch, k].wait_recv()
+        cols = chunk_cols(side, ch)
+        tpart[side, :, cols] = dot(gives[side], back[side, :, cols]).astype(BF16)
+        for k in range(N - 1, 0, -1):
+            at = pl.ds(k * TOK, TOK)
+            back2.append(
+                start(
+                    remote(
+                        tpart.at[side, at, cols], trecv.at[side, at, cols],
+                        c2s.at[side, ch, k - 1], c2r.at[side, ch, k - 1], along(side, N - OFF[k]),
+                    )
+                )
+            )
+        trecv[side, 0:TOK, cols] = tpart[side, 0:TOK, cols]
+
+    shards(4)
+    send_back(0, 0)
+    gbub_b[...] = dot(swap, gbub[...]).astype(BF16)
+    send_back(1, 0)
 
     towards = (ahead, behind)
     halves = (pl.ds(0, 64), pl.ds(64, 64))
@@ -258,34 +304,11 @@
                 remote(ring1_s.at[w, m], ring1_r.at[w, m], rs.at[w, 0, m], rr.at[w, 0, m], towards[w])
             )
 
-    for n in (2, 6, 1, 7, 0):
+    for n in (3, 5):
         shards(n)
-
-    line = N * SLOT
-    widths = (HALF + EXTRA, HALF)
-    back1 = []
-    for side in range(2):
-        mine = gbub if side == 0 else gbub_b
-
-        def tile_c(n, carry, side=side, mine=mine):
-            cols = pl.ds(pl.multiple_of(n * 256, 256), 256)
-            w_rows = pl.ds(pl.multiple_of(side * HALF + n * 256, 256), 256)
-            contrib[side, :, cols] = dot(mine[...], wgu[w_rows, :], 1, 1).astype(BF16)
-            return carry
-
-        lax.fori_loop(0, HALF // 256, tile_c, 0)
-        cols = pl.ds(0, widths[side])
-        for k in range(N - 1, 0, -1):
-            at = pl.ds(k * line, line)
-            back1.append(
-                start(
-                    remote(
-                        contrib.at[side, at, cols], back.at[side, at, cols],
-                        c1s.at[side, k - 1], c1r.at[side, k - 1], along(1 - side, N - OFF[k]),
-                    )
-                )
-            )
-        back[side, 0:line, cols] = contrib[side, 0:line, cols]
+    for ch in range(1, CHUNKS):
+        for side in range(2):
+            send_back(side, ch)
 
     def ring_step(step):
         swap_core[4 - step].wait_recv()
@@ -308,32 +331,17 @@
                 )
 
     ring_step(1)
+    for n in (2, 6, 1, 7, 0):
+        shards(n)
     ring_step(2)
-
-    for copy in back1:
-        copy.wait_recv()
-    back_2 = []
     for side in range(2):
-        for n in range(HALF // 256 + (side == 0)):
-            size = 256 if n < HALF // 256 else EXTRA
-            cols = pl.ds(n * 256, size)
-            tpart[side, :, cols] = dot(gives[side], back[side, :, cols]).astype(BF16)
-        cols = pl.ds(0, widths[side])
-        for k in range(N - 1, 0, -1):
-            at = pl.ds(k * TOK, TOK)
-            back_2.append(
-                start(
-                    remote(
-                        tpart.at[side, at, cols], trecv.at[side, at, cols],
-                        c2s.at[side, k - 1], c2r.at[side, k - 1], along(side, N - OFF[k]),
-                    )
-                )
-            )
-        trecv[side, 0:TOK, cols] = tpart[side, 0:TOK, cols]
-
+        send_home(side, 0)
     ring_step(3)
-
-    for copy in back_2:
+    for ch in range(1, CHUNKS):
+        for side in range(2):
+            send_home(side, ch)
+
+    for copy in back2:
         copy.wait_recv()
     for side in range(2):
         total = jnp.zeros((TOK, HALF), F32)
@@ -406,8 +414,8 @@
             dma((3,)),
             dma((2, N)), dma((2, N)),
             dma((2, GROUPS, N - 1)), dma((2, GROUPS, N - 1)),
-            dma((2, N - 1)), dma((2, N - 1)),
-            dma((2, N - 1)), dma((2, N - 1)),
+            dma((2, CHUNKS, N - 1)), dma((2, CHUNKS, N - 1)),
+            dma((2, CHUNKS, N - 1)), dma((2, CHUNKS, N - 1)),
             dma((N,)), dma((N,)),
             dma((2, 4, 3)), dma((2, 4, 3)),
         ],

time: 94.1 us -> 91.4 us (0.971)
  Pallas kernels: 93.3 us -> 89.8 us
    pallas_call x1, Pallas kernels: 92.4 us -> 88.9 us  [body(): pl.pallas_call(kernel, out_shape=(token_grad, jax.ShapeDtypeStruct(small,...]
where the time goes in v4:
time: 91.4 us; the launch traced here: 90.4 us
  Pallas kernels  89.8 us (98%)
    pallas_call x1, Pallas kernels, body(): pl.pallas_call(kernel, out_shape=(token_grad, jax.ShapeDtypeStruct(small,...  88.9 us

profile of v4, /device:TPU:1, one launch (start us, length us, event | category | flops | bytes accessed | tf_op | source)
XLA Modules:
  0.0 90.4 jit_solution(10624268391480487457)
XLA Ops:
  0.6 88.9 %expert_layer_backward.1 = (bf16[16,2048]{1,0:T(8,128)(2,1)S(1)}, f32[8,16]{1,0:T(8,128)S(1)}, f32[3,128,384]{2,1,0:T(8,128)S(1)}) custom-call(bf16[16,2048]{1,0:T(8,128)(2,1)} %tok_h.1, bf16[16,2048]{1,0:T(8,128)(2,1)} %dy_h.1, s32[8,16]{1,0:T(8,128)} %bitcast.3, bf16[8,16]{1,0:T(8,128)(2,1)} %bitcast.4, bf16[1,2048,384]{2,1,0:T(8,128)(2,1)} %wg_h.1, ...), custom_call_target="tpu_custom_call" | custom-call | tf_op jit(solution)/shard_map/expert_layer_backward/pallas_call | solution.py:385
  89.5 0.9 write_outputs.1
